TPU v7x, 32 devices: a whole 2x2x4 slice. The times are simulated.
32 devices in a mesh: member: 2 (over x), lat: 16 (over z, y, core).
Axes of the slice: x: 2, y: 2, z: 4, core: 2. Of those that a mesh axis runs over, the one named last changes fastest.
Arguments:
- height: float32 [128, 32, 1440], P(('member', 'lat')), parts along dimension 0, may hold values from -6 to 6
- zonal_courant: float32 [128, 32, 1440], P(('member', 'lat')), parts along dimension 0, may hold values from -1.5 to 1.5
- merid_courant: float32 [128, 32, 1440], P(('member', 'lat')), parts along dimension 0, may hold values from -1.5 to 1.5
- rates: float32 [64], P('member'), parts along dimension 0, may hold values from 0.05 to 0.5
- thresholds: float32 [64], P('member'), parts along dimension 0, may hold values from -3 to 3
- flags: int32 [64], replicated, may hold values from 0 to 1, as said below
- cutoffs: int32 [64], replicated, may hold values from 45 to 360
Outputs:
- filtered_height: float32 [128, 32, 1440], P(('member', 'lat')), parts along dimension 0
There are 2 independent parts, one for each index of `member`. A program takes and returns all parts, laid end to end along the dimension named above; an argument that names none is the same for every part. Nothing has to cross between parts.
Inputs may be any that keep to these rules, and one draw needn't show every extreme that they name: flags is 1 on a southern band of rows that starts at row 0 and on a northern band that ends at row 63, each band 64 // 8 to 16 rows long, and 0 on all other rows.
All inputs are finite; a program needn't handle non-finite values.
Results may differ from a plain program's by a relative error of at most 0.00007.
Values sent between devices are 32-bit elements; how exact they have to be, the bound alone decides.
No kernel may reach another device: no remote copies, remote signals or barrier semaphores. Data moves between devices by JAX's collectives and lax.ppermute only.
A program may use at most 64 MiB of HBM per device.

v0:
```python
import jax
import jax.numpy as jnp
from jax import lax
from jax.sharding import PartitionSpec as P


def padded_2(cells, sides, width):
    for axis, dim in sides:
        count = lax.axis_size(axis)
        ends = count - 1
        head = lax.slice_in_dim(cells, 0, width, axis=dim)
        tail = lax.slice_in_dim(cells, cells.shape[dim] - width, cells.shape[dim], axis=dim)
        cells = jnp.concatenate(
            [
                lax.ppermute(tail, axis, [(i, (i + 1) % count) for i in range(ends)]),
                cells,
                lax.ppermute(head, axis, [((i + 1) % count, i) for i in range(ends)]),
            ],
            axis=dim,
        )
    return cells


def transform_table(nlon, nkp):
    points = jnp.arange(nlon, dtype=jnp.int32)
    waves = jnp.arange(nkp, dtype=jnp.int32)
    phase = points[:, None] * waves[None, :] % nlon
    angle = 2.0 * jnp.pi / nlon * phase.astype(jnp.float32)
    return jnp.concatenate([jnp.cos(angle), jnp.sin(angle)], axis=1)


def wave_weights(nlon, nkp):
    waves = jnp.arange(nkp, dtype=jnp.int32)
    interior = jnp.where((waves > 0) & (waves < nlon // 2), 2.0, 1.0)
    return jnp.where(waves <= nlon // 2, interior, 0.0).astype(jnp.float32) / nlon


def damping(row_flags, row_cutoffs, nkp):
    waves = jnp.maximum(jnp.arange(nkp), 1).astype(jnp.float32)
    ratio = row_cutoffs.astype(jnp.float32)[:, None] / waves[None, :]
    factor = jnp.minimum(1.0, ratio * ratio)
    return jnp.where(row_flags[:, None] > 0, factor, 1.0)


def filter_units(flat, damp, table, weights):
    highest = lax.Precision.HIGHEST
    spectrum = jnp.dot(flat, table, precision=highest, preferred_element_type=jnp.float32)
    factor = (1.0 - damp) * weights[None, :]
    scaled = spectrum * jnp.concatenate([factor, factor], axis=1)
    dims = (((1,), (1,)), ((), ()))
    removed = lax.dot_general(
        scaled, table, dims, precision=highest, preferred_element_type=jnp.float32
    )
    return flat - removed


def filtered_or_kept(block, row_flags, row_cutoffs, table, weights):
    rows, levels, nlon = block.shape
    damp = damping(row_flags, row_cutoffs, weights.shape[0])
    unit_damp = jnp.broadcast_to(damp[:, None, :], (rows, levels, damp.shape[1])).reshape(
        rows * levels, damp.shape[1]
    )

    def apply_filter(data):
        return filter_units(data.reshape(rows * levels, nlon), unit_damp, table, weights).reshape(
            rows, levels, nlon
        )

    def keep_block(data):
        return data

    return lax.cond(jnp.any(row_flags > 0), apply_filter, keep_block, block)


def face_fluxes(rows_height, rows_speed, face_cos, count):
    face_value = (
        7.0 * (rows_height[1 : count + 1] + rows_height[2 : count + 2])
        - (rows_height[0:count] + rows_height[3 : count + 3])
    ) / 12.0
    speed = 0.5 * (rows_speed[0:count] + rows_speed[1 : count + 1]) * face_cos[:, None, None]
    return speed * face_value


def face_cosines(face_ids, nlat):
    return jnp.where(
        (face_ids > 0) & (face_ids < nlat),
        jnp.sin(jnp.pi * face_ids.astype(jnp.float32) / nlat),
        jnp.float32(0.0),
    )


def local(height, zonal_courant, merid_courant, rates, thresholds, flags, cutoffs):
    lat_rows, levels, nlon = height.shape
    devices = lax.axis_size("lat")
    position = lax.axis_index("lat")
    first_row = position * lat_rows
    nlat = lat_rows * devices
    local_rows = first_row + jnp.arange(lat_rows, dtype=jnp.int32)
    cos_rows = jnp.sin(jnp.pi * (local_rows.astype(jnp.float32) + 0.5) / nlat)
    faces = first_row + jnp.arange(lat_rows + 1, dtype=jnp.int32)
    cos_faces = face_cosines(faces, nlat)
    padded = padded_2(jnp.stack([height, merid_courant]), (("lat", 1),), 2)
    east = jnp.roll(height, -1, axis=2)
    west = jnp.roll(height, 1, axis=2)
    far_east = jnp.roll(height, -2, axis=2)
    face_height = (7.0 * (height + east) - (west + far_east)) / 12.0
    face_speed = 0.5 * (zonal_courant + jnp.roll(zonal_courant, -1, axis=2))
    zonal_flux = face_speed * face_height
    zonal_div = zonal_flux - jnp.roll(zonal_flux, 1, axis=2)
    source = -rates[None, :, None] * jax.nn.softplus(height - thresholds[None, :, None])
    partial_sums = jnp.sum(jnp.sum(source, axis=2) * cos_rows[:, None], axis=0)
    totals = lax.psum(partial_sums, "lat")
    all_rows = jnp.arange(nlat, dtype=jnp.int32)
    area = nlon * jnp.sum(jnp.sin(jnp.pi * (all_rows.astype(jnp.float32) + 0.5) / nlat))
    level_mean = totals / area
    padded_height = padded[0]
    padded_speed = padded[1]
    count = lat_rows + 1
    merid_flux = face_fluxes(padded_height, padded_speed[1:], cos_faces, count)
    merid_div = (merid_flux[1:] - merid_flux[:-1]) / cos_rows[:, None, None]
    updated = height - zonal_div - merid_div + source - level_mean[None, :, None]
    nkp = (nlon // 2 + 128) // 128 * 128
    table = transform_table(nlon, nkp)
    weights = wave_weights(nlon, nkp)
    row_flags = lax.dynamic_slice_in_dim(flags, first_row, lat_rows)
    row_cutoffs = lax.dynamic_slice_in_dim(cutoffs, first_row, lat_rows)
    result = filtered_or_kept(updated, row_flags, row_cutoffs, table, weights)
    return result


def solution(mesh):
    return jax.shard_map(
        local,
        mesh=mesh,
        in_specs=(
            P(("member", "lat"), None, None),
            P(("member", "lat"), None, None),
            P(("member", "lat"), None, None),
            P("member"),
            P("member"),
            P(),
            P(),
        ),
        out_specs=P(("member", "lat"), None, None),
        check_vma=False,
    )
```

profile of v0, /device:TPU:0, one launch (start us, length us, event | category | flops | bytes accessed | tf_op | source)
XLA Modules:
  0.0 101.5 jit_solution(3019089762479028692)
XLA Ops:
  0.0 2.8 %fusion.17 = (f32[2,2,32,1440]{3,2,1,0:T(8,128)}, f32[2,2,32,1440]{3,2,1,0:T(8,128)}) fusion(f32[1,4,32,1440]{3,2,1,0:T(8,128)} %bitcast.21, f32[1,4,32,1440]{3,2,1,0:T(8,128)} %bitcast.27), kind=kLoop, calls=%fused_computation.33 | loop fusion | flops 368640 | bytes 2949120 | tf_op jit(solution)/shard_map/stack | solution.py:102
  2.8 3.3 %collective-permute-start = (f32[2,2,32,1440]{3,2,1,0:T(8,128)}, f32[2,2,32,1440]{3,2,1,0:T(8,128)}, u32[]{:S(2)}, u32[]{:S(2)}) collective-permute-start(f32[2,2,32,1440]{3,2,1,0:T(8,128)} %get-tuple-element.115), channel_id=1, source_target_pairs={{0,1},{1,2},{2,3},{3,4},{4,5},{5,6},{6,7},{7,8},{8,9},{9,10},{10,1... | collective-permute-start | bytes 2211848 | tf_op jit(solution)/shard_map/ppermute | solution.py:15
  6.1 1.3 %collective-permute-start.1 = (f32[2,2,32,1440]{3,2,1,0:T(8,128)}, f32[2,2,32,1440]{3,2,1,0:T(8,128)}, u32[]{:S(2)}, u32[]{:S(2)}) collective-permute-start(f32[2,2,32,1440]{3,2,1,0:T(8,128)} %get-tuple-element.116), channel_id=1, source_target_pairs={{1,0},{2,1},{3,2},{4,3},{5,4},{6,5},{7,6},{8,7},{9,8},{10,9},{11,1... | collective-permute-start | bytes 2211848 | tf_op jit(solution)/shard_map/ppermute | solution.py:17
  7.3 2.8 %fusion.33 = (f32[4,32,1439]{2,1,0:T(8,128)}, f32[4,32,1439]{2,1,0:T(8,128)}) fusion(f32[4,32,1440]{2,1,0:T(8,128)} %param.9), kind=kLoop, calls=%fused_computation.63 | loop fusion | bytes 2947072 | tf_op jit(solution)/shard_map/jit(_roll_static)/slice | solution.py:104
  10.1 0.1 fusion.32
  10.2 0.3 slice.95
  10.5 1.2 %slice.89 = f32[4,32,1439]{2,1,0:T(8,128)} slice(f32[4,32,1440]{2,1,0:T(8,128)S(1)} %copy-done.2), slice={[0:4], [0:32], [1:1440]} | slice | bytes 1473536 | tf_op jit(solution)/shard_map/jit(_roll_static)/slice | solution.py:107
  11.8 0.7 sine_reduce_fusion
  12.5 19.6 %fusion.7 = (f32[1440,768]{1,0:T(8,128)}, f32[1440,768]{1,0:T(8,128)}) fusion(), kind=kLoop, calls=%fused_computation.15 | loop fusion | flops 9953280 | bytes 8847360 | tf_op jit(solution)/shard_map/sin | solution.py:29
  32.1 0.9 fusion.29
  33.0 0.1 multiply_reduce_fusion
  33.1 35.8 %psum.7 = f32[32]{0:T(128)S(1)} all-reduce(f32[32]{0:T(128)S(1)} %multiply_reduce_fusion), channel_id=1, replica_groups=mesh['member'=2,'lat'=16] {'lat'}, use_global_device_ids=true, to_apply=%region_3.4 | all-reduce | flops 32 | bytes 256 | tf_op jit(solution)/shard_map/psum | solution.py:112
  68.9 0.1 slice.109
  69.0 0.8 fusion.31
  71.2 8.2 %pad_maximum_fusion = f32[1440,1536]{1,0:T(8,128)} fusion(f32[1440,768]{1,0:T(8,128)} %get-tuple-element.123, f32[1440,768]{1,0:T(8,128)} %get-tuple-element.124), kind=kLoop, calls=%fused_computation.8 | loop fusion | flops 2211840 | bytes 17694720 | tf_op jit(solution)/shard_map/concatenate | solution.py:29
  79.4 1.9 %maximum_maximum_fusion = (f32[2,6,32,1440]{3,2,1,0:T(8,128)S(1)}, f32[2,6,32,1440]{3,2,1,0:T(8,128)S(1)}) fusion(f32[1,4,32,1440]{3,2,1,0:T(8,128)S(1)} %bitcast.28, f32[1,4,32,1440]{3,2,1,0:T(8,128)S(1)} %bitcast.22, f32[2,2,32,1440]{3,2,1,0:T(8,128)} %collective-permute-done, f32[2,2,32,1440]{3,2,1,0:T(8,128)} %collective-permute-done.1), kind=kLoop, calls=%fused_computation.18 | loop fusion | flops 2211840 | bytes 7372800 | tf_op jit(solution)/shard_map/concatenate | solution.py:13
  81.3 0.5 fusion.13
  81.8 0.7 fusion.22
  82.6 18.0 %conditional.1 = (f32[4,32,1440]{2,1,0:T(8,128)S(1)}) conditional(s32[]{:T(128)} %convert_element_type.42, f32[4,32,1440]{2,1,0:T(8,128)S(1)} %fusion.22, (f32[4,32,1440]{2,1,0:T(8,128)S(1)}, f32[1440,1536]{1,0:T(8,128)}, pred[4]{0:T(512)(128)(4,1)S(1)}, f32[4]{0:T(128)S(1)}, f32[1,768]{1,0:T(1,128)S(1)}, /*index=5*/s32[768]{0:T(1024)S(1)}) %tuple.45), branch_computations={%region_5.6_spmd, %region_6.7_spmd} | conditional | flops 6795468800 | bytes 25258016 | solution.py:72
  82.9 7.6 %convolution_multiply_fusion = f32[128,1536]{1,0:T(8,128)S(1)} fusion(f32[128,1440]{1,0:T(8,128)S(1)} %bitcast.24, f32[1440,1536]{1,0:T(8,128)} %get-tuple-element.105, f32[128,768]{1,0:T(8,128)S(1)} %bitcast_multiply_fusion), kind=kOutput, calls=%fused_computation.1 | convolution fusion | flops 3397779456 | bytes 10764288 | tf_op jit(solution)/shard_map/cond/branch_1_fun/dot_general | solution.py:47
  90.6 0.3 copy.27
  90.8 9.5 %convolution_subtract_fusion = f32[128,1440]{0,1:T(8,128)S(1)} fusion(f32[128,1440]{0,1:T(8,128)S(1)} %copy.27, f32[128,1536]{1,0:T(8,128)S(1)} %convolution_multiply_fusion, f32[1440,1536]{1,0:T(8,128)} %get-tuple-element.105), kind=kOutput, calls=%fused_computation | convolution fusion | flops 3397570560 | bytes 11108352 | tf_op jit(solution)/shard_map/cond/branch_1_fun/dot_general | solution.py:51
  100.3 0.3 copy.28
  100.6 0.9 copy-done.1
  (37 shorter events, 0.4 us)
Async XLA Ops:
  0.0 10.1 %copy-start = (f32[4,32,1440]{2,1,0:T(8,128)S(1)}, f32[4,32,1440]{2,1,0:T(8,128)}, u32[]{:S(2)}) copy-start(f32[4,32,1440]{2,1,0:T(8,128)} %param.9) | copy-start | bytes 2211844
  0.0 10.5 %copy-start.2 = (f32[4,32,1440]{2,1,0:T(8,128)S(1)}, f32[4,32,1440]{2,1,0:T(8,128)}, u32[]{:S(2)}) copy-start(f32[4,32,1440]{2,1,0:T(8,128)} %param.10) | copy-start | bytes 2211844
  2.8 76.6 %collective-permute-start = (f32[2,2,32,1440]{3,2,1,0:T(8,128)}, f32[2,2,32,1440]{3,2,1,0:T(8,128)}, u32[]{:S(2)}, u32[]{:S(2)}) collective-permute-start(f32[2,2,32,1440]{3,2,1,0:T(8,128)} %get-tuple-element.115), channel_id=1, source_target_pairs={{0,1},{1,2},{2,3},{3,4},{4,5},{5,6},{6,7},{7,8},{8,9},{9,10},{10,1... | collective-permute-start | bytes 2211848 | tf_op jit(solution)/shard_map/ppermute | solution.py:15
  6.1 73.3 %collective-permute-start.1 = (f32[2,2,32,1440]{3,2,1,0:T(8,128)}, f32[2,2,32,1440]{3,2,1,0:T(8,128)}, u32[]{:S(2)}, u32[]{:S(2)}) collective-permute-start(f32[2,2,32,1440]{3,2,1,0:T(8,128)} %get-tuple-element.116), channel_id=1, source_target_pairs={{1,0},{2,1},{3,2},{4,3},{5,4},{6,5},{7,6},{8,7},{9,8},{10,9},{11,1... | collective-permute-start | bytes 2211848 | tf_op jit(solution)/shard_map/ppermute | solution.py:17
  12.4 19.6 %copy-start.9 = (f32[32]{0:T(128)S(1)}, f32[32]{0:T(128)}, u32[]{:S(2)}) copy-start(f32[32]{0:T(128)} %param.12) | copy-start | bytes 388
  12.4 19.6 %slice-start = ((f32[4,32,1440]{2,1,0:T(8,128)}), f32[4,32,1]{2,1,0:T(8,128)S(1)}, s32[]{:S(2)}) async-start(f32[4,32,1440]{2,1,0:T(8,128)} %param.10), calls=%async_computation | async-start | bytes 131072 | tf_op jit(solution)/shard_map/jit(_roll_static)/slice | solution.py:107
  12.4 19.7 %copy-start.3 = (f32[4,32,1439]{2,1,0:T(8,128)S(1)}, f32[4,32,1439]{2,1,0:T(8,128)}, u32[]{:S(2)}) copy-start(f32[4,32,1439]{2,1,0:T(8,128)} %slice.89) | copy-start | bytes 2210308
  12.4 19.7 %copy-start.4 = (f32[4,32,1439]{2,1,0:T(8,128)S(1)}, f32[4,32,1439]{2,1,0:T(8,128)}, u32[]{:S(2)}) copy-start(f32[4,32,1439]{2,1,0:T(8,128)} %get-tuple-element.121) | copy-start | bytes 2210308
  12.4 19.7 %copy-start.5 = (f32[4,32,1439]{2,1,0:T(8,128)S(1)}, f32[4,32,1439]{2,1,0:T(8,128)}, u32[]{:S(2)}) copy-start(f32[4,32,1439]{2,1,0:T(8,128)} %get-tuple-element.122) | copy-start | bytes 2210308
  12.4 19.7 %copy-start.7 = (f32[32]{0:T(128)S(1)}, f32[32]{0:T(128)}, u32[]{:S(2)}) copy-start(f32[32]{0:T(128)} %param.13) | copy-start | bytes 388
  32.0 37.0 %copy-start.8 = (s32[64]{0:T(128)S(1)}, s32[64]{0:T(128)}, u32[]{:S(2)}) copy-start(s32[64]{0:T(128)} %param.14) | copy-start | bytes 772
  32.0 37.8 %copy-start.10 = (s32[64]{0:T(128)S(1)}, s32[64]{0:T(128)}, u32[]{:S(2)}) copy-start(s32[64]{0:T(128)} %param.15) | copy-start | bytes 772
  71.2 8.2 %copy-start.6 = (f32[4,32,1440]{2,1,0:T(8,128)S(1)}, f32[4,32,1440]{2,1,0:T(8,128)}, u32[]{:S(2)}) copy-start(f32[4,32,1440]{2,1,0:T(8,128)} %param.11) | copy-start | bytes 2211844
  100.6 0.9 copy-start.1
where the time goes:
time: 102 us; the launch traced here: 101 us
  other arithmetic  36.4 us (36%)
  blocking collectives  35.8 us (35%)
  matrix products  17.1 us (17%)
  local copies, waits for them, and re-layouts  5.82 us (6%)
  starting transfers between devices  4.55 us (4%)
  between operations  1.52 us (1%)
    psum x1, blocking collectives, local(): totals = lax.psum(partial_sums, 'lat')  35.8 us
    sin x1, other arithmetic, transform_table(): return jnp.concatenate([jnp.cos(angle), jnp.sin(angle)], axis=1)  19.6 us
    dot_general x1, matrix products, filter_units(): lax.dot_general(scaled, table, dims, precision=highest, preferred_element...  9.48 us
    concatenate x1, other arithmetic, transform_table(): return jnp.concatenate([jnp.cos(angle), jnp.sin(angle)], axis=1)  8.16 us
    dot_general x1, matrix products, filter_units(): jnp.dot(flat, table, precision=highest, preferred_element_type=jnp.float32)  7.64 us
    ppermute x1, starting transfers between devices, padded_2(): lax.ppermute(tail, axis, [(i, (i + 1) % count) for i in range(ends)])  3.27 us
    slice x2, local copies, waits for them, and re-layouts, local(): west = jnp.roll(height, 1, axis=2)  2.85 us
    another operation x1, other arithmetic, local(): padded = padded_2(jnp.stack([height, merid_courant]), (('lat', 1),), 2)  2.78 us
  transfers between devices with their start and end apart: 2, of which 0 were waited for; matrix products, arithmetic and copies ran while one was open for 34% of the time, Pallas kernels for 0%

commit v1 on v0

--- a/solution.py
+++ b/solution.py
@@ -109,7 +109,11 @@
     zonal_div = zonal_flux - jnp.roll(zonal_flux, 1, axis=2)
     source = -rates[None, :, None] * jax.nn.softplus(height - thresholds[None, :, None])
     partial_sums = jnp.sum(jnp.sum(source, axis=2) * cos_rows[:, None], axis=0)
-    totals = lax.psum(partial_sums, "lat")
+    n_dev_all = jax.lax.psum(1, "lat")
+    totals = partial_sums
+    for to_i in [src_i for src_i in (1, 2, 4, 8, 16) if src_i < n_dev_all]:
+        m_next = jax.lax.ppermute(totals, "lat", [(s, s ^ to_i) for s in range(n_dev_all)])
+        totals = totals + m_next
     all_rows = jnp.arange(nlat, dtype=jnp.int32)
     area = nlon * jnp.sum(jnp.sin(jnp.pi * (all_rows.astype(jnp.float32) + 0.5) / nlat))
     level_mean = totals / area

time: 102 us -> 81.8 us (0.80)
  blocking collectives: 35.8 us -> 0 us
  starting transfers between devices: 4.55 us -> 14.7 us
  waiting for transfers between devices: 0.01 us -> 2.8 us
  local copies, waits for them, and re-layouts: 5.82 us -> 7.93 us
    psum x1 -> x0, blocking collectives: 35.8 us -> none  [local(): totals = lax.psum(partial_sums, 'lat')]
    ppermute x0 -> x4, starting transfers between devices: none -> 10.5 us  [local(): jax.lax.ppermute(totals, 'lat', [(s, s ^ to_i) for s in range(n_dev_all)])]
    ppermute x0 -> x4, waiting for transfers between devices: none -> 2.79 us  [local(): jax.lax.ppermute(totals, 'lat', [(s, s ^ to_i) for s in range(n_dev_all)])]
    reduce_sum x2, other arithmetic: 1 us -> 2.59 us  [local(): partial_sums = jnp.sum(jnp.sum(source, axis=2) * cos_rows[:, None], axis=0)]
    slice x2 -> x3, local copies, waits for them, and re-layouts: 0.28 us -> 1.41 us  [local(): far_east = jnp.roll(height, -2, axis=2)]
  transfers between devices with their start and end apart: 2 -> 6, of which waited for: 0 -> 3; matrix products, arithmetic and copies ran while one was open for 34% -> 39% of each run, Pallas kernels for 0% -> 0%
where the time goes in v1:
time: 81.8 us; the launch traced here: 81.4 us
  other arithmetic  37.3 us (46%)
  matrix products  17.1 us (21%)
  starting transfers between devices  14.7 us (18%)
  local copies, waits for them, and re-layouts  7.93 us (10%)
  waiting for transfers between devices  2.8 us (3%)
  between operations  1.41 us (2%)
    sin x1, other arithmetic, transform_table(): return jnp.concatenate([jnp.cos(angle), jnp.sin(angle)], axis=1)  19.5 us
    ppermute x4, starting transfers between devices, local(): jax.lax.ppermute(totals, 'lat', [(s, s ^ to_i) for s in range(n_dev_all)])  10.5 us
    dot_general x1, matrix products, filter_units(): lax.dot_general(scaled, table, dims, precision=highest, preferred_element...  9.49 us
    concatenate x1, other arithmetic, transform_table(): return jnp.concatenate([jnp.cos(angle), jnp.sin(angle)], axis=1)  8.17 us
    dot_general x1, matrix products, filter_units(): jnp.dot(flat, table, precision=highest, preferred_element_type=jnp.float32)  7.6 us
    slice x2, local copies, waits for them, and re-layouts, local(): west = jnp.roll(height, 1, axis=2)  3.84 us
    ppermute x1, starting transfers between devices, padded_2(): lax.ppermute(tail, axis, [(i, (i + 1) % count) for i in range(ends)])  2.84 us
    ppermute x4, waiting for transfers between devices, local(): jax.lax.ppermute(totals, 'lat', [(s, s ^ to_i) for s in range(n_dev_all)])  2.79 us
  transfers between devices with their start and end apart: 6, of which 3 were waited for; matrix products, arithmetic and copies ran while one was open for 39% of the time, Pallas kernels for 0%

profile of v1, /device:TPU:0, one launch (start us, length us, event | category | flops | bytes accessed | tf_op | source)
XLA Modules:
  0.0 81.4 jit_solution(8887443526449307695)
XLA Ops:
  0.0 2.9 %fusion.33 = (f32[4,32,1439]{2,1,0:T(8,128)}, f32[4,32,1439]{2,1,0:T(8,128)}) fusion(f32[4,32,1440]{2,1,0:T(8,128)} %param.9), kind=kLoop, calls=%fused_computation.63 | loop fusion | bytes 2947072 | tf_op jit(solution)/shard_map/jit(_roll_static)/slice | solution.py:104
  2.9 1.0 %fusion.32 = (f32[4,32,1]{2,1,0:T(8,128)S(1)}, f32[4,32,1]{2,1,0:T(8,128)S(1)}) fusion(f32[4,32,1440]{2,1,0:T(8,128)} %param.9), kind=kLoop, calls=%fused_computation.62 | loop fusion | bytes 2048 | tf_op jit(solution)/shard_map/jit(_roll_static)/slice | solution.py:104
  3.9 1.4 %slice.95 = f32[4,32,1438]{2,1,0:T(8,128)S(1)} slice(f32[4,32,1440]{2,1,0:T(8,128)} %param.9), slice={[0:4], [0:32], [2:1440]} | slice | bytes 1472512 | tf_op jit(solution)/shard_map/jit(_roll_static)/slice | solution.py:105
  5.3 1.2 %slice.89 = f32[4,32,1439]{2,1,0:T(8,128)} slice(f32[4,32,1440]{2,1,0:T(8,128)S(1)} %copy-done.2), slice={[0:4], [0:32], [1:1440]} | slice | bytes 1473536 | tf_op jit(solution)/shard_map/jit(_roll_static)/slice | solution.py:107
  6.5 2.5 %fusion.29 = (f32[4,32]{1,0:T(4,128)S(1)}, f32[4,32,1440]{2,1,0:T(8,128)S(1)}) fusion(f32[4,32,1440]{2,1,0:T(8,128)S(1)} %copy-done, f32[32]{0:T(128)S(1)} %copy-done.4, f32[32]{0:T(128)S(1)} %neg.8, f32[4,32,2]{2,1,0:T(8,128)S(1)} %slice-done, f32[4,32,1438]{2,1,0:T(8,128)S(1)} %slice.95, f32[4,32,1439]{2,1,0:T(8,128)} %get-tuple-element.121, ...), kind=kLoop, calls=%fused_computation.51 | loop fusion | flops 3870592 | bytes 5161728 | tf_op jit(solution)/shard_map/reduce_sum | solution.py:111
  9.6 2.1 %fusion.17 = (f32[2,2,32,1440]{3,2,1,0:T(8,128)}, f32[2,2,32,1440]{3,2,1,0:T(8,128)S(1)}) fusion(f32[1,4,32,1440]{3,2,1,0:T(8,128)S(1)} %bitcast.21, f32[1,4,32,1440]{3,2,1,0:T(8,128)} %bitcast.27), kind=kLoop, calls=%fused_computation.33 | loop fusion | flops 368640 | bytes 2949120 | tf_op jit(solution)/shard_map/stack | solution.py:102
  11.8 2.8 %collective-permute-start = (f32[2,2,32,1440]{3,2,1,0:T(8,128)}, f32[2,2,32,1440]{3,2,1,0:T(8,128)}, u32[]{:S(2)}, u32[]{:S(2)}) collective-permute-start(f32[2,2,32,1440]{3,2,1,0:T(8,128)} %get-tuple-element.115), channel_id=1, source_target_pairs={{0,1},{1,2},{2,3},{3,4},{4,5},{5,6},{6,7},{7,8},{8,9},{9,10},{10,1... | collective-permute-start | bytes 2211848 | tf_op jit(solution)/shard_map/ppermute | solution.py:15
  14.6 1.3 %collective-permute-start.1 = (f32[2,2,32,1440]{3,2,1,0:T(8,128)S(1)}, f32[2,2,32,1440]{3,2,1,0:T(8,128)}, u32[]{:S(2)}, u32[]{:S(2)}) collective-permute-start(f32[2,2,32,1440]{3,2,1,0:T(8,128)S(1)} %get-tuple-element.116), channel_id=1, source_target_pairs={{1,0},{2,1},{3,2},{4,3},{5,4},{6,5},{7,6},{8,7},{9,8},{10,9},{11,1... | collective-permute-start | bytes 2211848 | tf_op jit(solution)/shard_map/ppermute | solution.py:17
  16.0 19.5 %fusion.7 = (f32[1440,768]{1,0:T(8,128)}, f32[1440,768]{1,0:T(8,128)}) fusion(), kind=kLoop, calls=%fused_computation.15 | loop fusion | flops 9953280 | bytes 8847360 | tf_op jit(solution)/shard_map/sin | solution.py:29
  35.5 0.8 fusion.31
  36.4 8.2 %pad_maximum_fusion = f32[1440,1536]{1,0:T(8,128)} fusion(f32[1440,768]{1,0:T(8,128)} %get-tuple-element.123, f32[1440,768]{1,0:T(8,128)} %get-tuple-element.124), kind=kLoop, calls=%fused_computation.8 | loop fusion | flops 2211840 | bytes 17694720 | tf_op jit(solution)/shard_map/concatenate | solution.py:29
  44.6 4.0 %collective-permute-start.3 = (f32[32]{0:T(128)S(1)}, f32[32]{0:T(128)S(1)}, u32[]{:S(2)}, u32[]{:S(2)}) collective-permute-start(f32[32]{0:T(128)S(1)} %add.110), channel_id=1, source_target_pairs={{0,2},{1,3},{2,0},{3,1},{4,6},{5,7},{6,4},{7,5},{8,10},{9,11},{10,... | collective-permute-start | bytes 392 | tf_op jit(solution)/shard_map/ppermute | solution.py:115
  49.3 0.9 %collective-permute-done.3 = f32[32]{0:T(128)S(1)} collective-permute-done((f32[32]{0:T(128)S(1)}, f32[32]{0:T(128)S(1)}, u32[]{:S(2)}, u32[]{:S(2)}) %collective-permute-start.3) | collective-permute-done | bytes 160 | tf_op jit(solution)/shard_map/ppermute | solution.py:115
  50.2 3.0 %collective-permute-start.4 = (f32[32]{0:T(128)S(1)}, f32[32]{0:T(128)S(1)}, u32[]{:S(2)}, u32[]{:S(2)}) collective-permute-start(f32[32]{0:T(128)S(1)} %add.111), channel_id=1, source_target_pairs={{0,4},{1,5},{2,6},{3,7},{4,0},{5,1},{6,2},{7,3},{8,12},{9,13},{10,... | collective-permute-start | bytes 392 | tf_op jit(solution)/shard_map/ppermute | solution.py:115
  53.2 0.6 sine_reduce_fusion
  53.8 0.9 %collective-permute-done.4 = f32[32]{0:T(128)S(1)} collective-permute-done((f32[32]{0:T(128)S(1)}, f32[32]{0:T(128)S(1)}, u32[]{:S(2)}, u32[]{:S(2)}) %collective-permute-start.4) | collective-permute-done | bytes 160 | tf_op jit(solution)/shard_map/ppermute | solution.py:115
  54.7 3.0 %collective-permute-start.5 = (f32[32]{0:T(128)S(1)}, f32[32]{0:T(128)S(1)}, u32[]{:S(2)}, u32[]{:S(2)}) collective-permute-start(f32[32]{0:T(128)S(1)} %add.112), channel_id=1, source_target_pairs={{0,8},{1,9},{2,10},{3,11},{4,12},{5,13},{6,14},{7,15},{8,0},{9,1},... | collective-permute-start | bytes 392 | tf_op jit(solution)/shard_map/ppermute | solution.py:115
  58.3 1.0 %collective-permute-done.5 = f32[32]{0:T(128)S(1)} collective-permute-done((f32[32]{0:T(128)S(1)}, f32[32]{0:T(128)S(1)}, u32[]{:S(2)}, u32[]{:S(2)}) %collective-permute-start.5) | collective-permute-done | bytes 160 | tf_op jit(solution)/shard_map/ppermute | solution.py:115
  59.3 1.9 %maximum_maximum_fusion = (f32[2,6,32,1440]{3,2,1,0:T(8,128)S(1)}, f32[2,6,32,1440]{3,2,1,0:T(8,128)S(1)}) fusion(f32[1,4,32,1440]{3,2,1,0:T(8,128)S(1)} %bitcast.28, f32[1,4,32,1440]{3,2,1,0:T(8,128)S(1)} %bitcast.22, f32[2,2,32,1440]{3,2,1,0:T(8,128)} %collective-permute-done, f32[2,2,32,1440]{3,2,1,0:T(8,128)} %collective-permute-done.1), kind=kLoop, calls=%fused_computation.18 | loop fusion | flops 2211840 | bytes 7372800 | tf_op jit(solution)/shard_map/concatenate | solution.py:13
  61.8 0.7 fusion.22
  62.5 18.0 %conditional.1 = (f32[4,32,1440]{2,1,0:T(8,128)S(1)}) conditional(s32[]{:T(128)} %convert_element_type.42, f32[4,32,1440]{2,1,0:T(8,128)S(1)} %fusion.22, (f32[4,32,1440]{2,1,0:T(8,128)S(1)}, f32[1440,1536]{1,0:T(8,128)}, pred[4]{0:T(512)(128)(4,1)S(1)}, f32[4]{0:T(128)S(1)}, f32[1,768]{1,0:T(1,128)S(1)}, /*index=5*/s32[768]{0:T(1024)S(1)}) %tuple.45), branch_computations={%region_4.5_spmd, %region_5.6_spmd} | conditional | flops 6795468800 | bytes 25258016 | solution.py:72
  62.9 7.6 %convolution_multiply_fusion = f32[128,1536]{1,0:T(8,128)S(1)} fusion(f32[128,1440]{1,0:T(8,128)S(1)} %bitcast.24, f32[1440,1536]{1,0:T(8,128)} %get-tuple-element.105, f32[128,768]{1,0:T(8,128)S(1)} %bitcast_multiply_fusion), kind=kOutput, calls=%fused_computation.1 | convolution fusion | flops 3397779456 | bytes 10764288 | tf_op jit(solution)/shard_map/cond/branch_1_fun/dot_general | solution.py:47
  70.8 9.5 %convolution_subtract_fusion = f32[128,1440]{0,1:T(8,128)S(1)} fusion(f32[128,1440]{0,1:T(8,128)S(1)} %copy.27, f32[128,1536]{1,0:T(8,128)S(1)} %convolution_multiply_fusion, f32[1440,1536]{1,0:T(8,128)} %get-tuple-element.105), kind=kOutput, calls=%fused_computation | convolution fusion | flops 3397570560 | bytes 11108352 | tf_op jit(solution)/shard_map/cond/branch_1_fun/dot_general | solution.py:51
  80.5 0.9 %copy-done.1 = f32[4,32,1440]{2,1,0:T(8,128)} copy-done((f32[4,32,1440]{2,1,0:T(8,128)}, f32[4,32,1440]{2,1,0:T(8,128)S(1)}, u32[]{:S(2)}) %copy-start.1) | copy-done | bytes 737304
  (42 shorter events, 2.1 us)
Async XLA Ops:
  0.0 6.5 %copy-start = (f32[4,32,1440]{2,1,0:T(8,128)S(1)}, f32[4,32,1440]{2,1,0:T(8,128)}, u32[]{:S(2)}) copy-start(f32[4,32,1440]{2,1,0:T(8,128)} %param.9) | copy-start | bytes 2211844
  0.0 6.5 %slice-start = ((f32[4,32,1440]{2,1,0:T(8,128)}), f32[4,32,2]{2,1,0:T(8,128)S(1)}, s32[]{:S(2)}) async-start(f32[4,32,1440]{2,1,0:T(8,128)} %param.9), calls=%async_computation | async-start | bytes 131072 | tf_op jit(solution)/shard_map/jit(_roll_static)/slice | solution.py:105
  0.0 5.3 %copy-start.2 = (f32[4,32,1440]{2,1,0:T(8,128)S(1)}, f32[4,32,1440]{2,1,0:T(8,128)}, u32[]{:S(2)}) copy-start(f32[4,32,1440]{2,1,0:T(8,128)} %param.10) | copy-start | bytes 2211844
  0.0 6.5 %slice-start.1 = ((f32[4,32,1440]{2,1,0:T(8,128)}), f32[4,32,1]{2,1,0:T(8,128)S(1)}, s32[]{:S(2)}) async-start(f32[4,32,1440]{2,1,0:T(8,128)} %param.10), calls=%async_computation.1 | async-start | bytes 131072 | tf_op jit(solution)/shard_map/jit(_roll_static)/slice | solution.py:107
  0.0 6.4 %copy-start.6 = (f32[32]{0:T(128)S(1)}, f32[32]{0:T(128)}, u32[]{:S(2)}) copy-start(f32[32]{0:T(128)} %param.12) | copy-start | bytes 388
  0.0 6.5 %copy-start.4 = (f32[32]{0:T(128)S(1)}, f32[32]{0:T(128)}, u32[]{:S(2)}) copy-start(f32[32]{0:T(128)} %param.13) | copy-start | bytes 388
  9.1 35.5 %collective-permute-start.2 = (f32[32]{0:T(128)S(1)}, f32[32]{0:T(128)S(1)}, u32[]{:S(2)}, u32[]{:S(2)}) collective-permute-start(f32[32]{0:T(128)S(1)} %multiply_reduce_fusion), channel_id=1, source_target_pairs={{0,1},{1,0},{2,3},{3,2},{4,5},{5,4},{6,7},{7,6},{8,9},{9,8},{10,11... | collective-permute-start | bytes 392 | tf_op jit(solution)/shard_map/ppermute | solution.py:115
  11.8 47.6 %collective-permute-start = (f32[2,2,32,1440]{3,2,1,0:T(8,128)}, f32[2,2,32,1440]{3,2,1,0:T(8,128)}, u32[]{:S(2)}, u32[]{:S(2)}) collective-permute-start(f32[2,2,32,1440]{3,2,1,0:T(8,128)} %get-tuple-element.115), channel_id=1, source_target_pairs={{0,1},{1,2},{2,3},{3,4},{4,5},{5,6},{6,7},{7,8},{8,9},{9,10},{10,1... | collective-permute-start | bytes 2211848 | tf_op jit(solution)/shard_map/ppermute | solution.py:15
  14.6 44.7 %collective-permute-start.1 = (f32[2,2,32,1440]{3,2,1,0:T(8,128)S(1)}, f32[2,2,32,1440]{3,2,1,0:T(8,128)}, u32[]{:S(2)}, u32[]{:S(2)}) collective-permute-start(f32[2,2,32,1440]{3,2,1,0:T(8,128)S(1)} %get-tuple-element.116), channel_id=1, source_target_pairs={{1,0},{2,1},{3,2},{4,3},{5,4},{6,5},{7,6},{8,7},{9,8},{10,9},{11,1... | collective-permute-start | bytes 2211848 | tf_op jit(solution)/shard_map/ppermute | solution.py:17
  15.9 19.6 %copy-start.5 = (s32[64]{0:T(128)S(1)}, s32[64]{0:T(128)}, u32[]{:S(2)}) copy-start(s32[64]{0:T(128)} %param.14) | copy-start | bytes 772
  15.9 20.3 %copy-start.7 = (s32[64]{0:T(128)S(1)}, s32[64]{0:T(128)}, u32[]{:S(2)}) copy-start(s32[64]{0:T(128)} %param.15) | copy-start | bytes 772
  36.4 23.0 %copy-start.3 = (f32[4,32,1440]{2,1,0:T(8,128)S(1)}, f32[4,32,1440]{2,1,0:T(8,128)}, u32[]{:S(2)}) copy-start(f32[4,32,1440]{2,1,0:T(8,128)} %param.11) | copy-start | bytes 2211844
  44.6 5.6 %collective-permute-start.3 = (f32[32]{0:T(128)S(1)}, f32[32]{0:T(128)S(1)}, u32[]{:S(2)}, u32[]{:S(2)}) collective-permute-start(f32[32]{0:T(128)S(1)} %add.110), channel_id=1, source_target_pairs={{0,2},{1,3},{2,0},{3,1},{4,6},{5,7},{6,4},{7,5},{8,10},{9,11},{10,... | collective-permute-start | bytes 392 | tf_op jit(solution)/shard_map/ppermute | solution.py:115
  50.2 4.5 %collective-permute-start.4 = (f32[32]{0:T(128)S(1)}, f32[32]{0:T(128)S(1)}, u32[]{:S(2)}, u32[]{:S(2)}) collective-permute-start(f32[32]{0:T(128)S(1)} %add.111), channel_id=1, source_target_pairs={{0,4},{1,5},{2,6},{3,7},{4,0},{5,1},{6,2},{7,3},{8,12},{9,13},{10,... | collective-permute-start | bytes 392 | tf_op jit(solution)/shard_map/ppermute | solution.py:115
  54.7 4.6 %collective-permute-start.5 = (f32[32]{0:T(128)S(1)}, f32[32]{0:T(128)S(1)}, u32[]{:S(2)}, u32[]{:S(2)}) collective-permute-start(f32[32]{0:T(128)S(1)} %add.112), channel_id=1, source_target_pairs={{0,8},{1,9},{2,10},{3,11},{4,12},{5,13},{6,14},{7,15},{8,0},{9,1},... | collective-permute-start | bytes 392 | tf_op jit(solution)/shard_map/ppermute | solution.py:115
  80.5 0.9 %copy-start.1 = (f32[4,32,1440]{2,1,0:T(8,128)}, f32[4,32,1440]{2,1,0:T(8,128)S(1)}, u32[]{:S(2)}) copy-start(f32[4,32,1440]{2,1,0:T(8,128)S(1)} %get-tuple-element.127) | copy-start | bytes 2211844
